TPU v7x, 128 devices: a whole 4x4x4 slice. The times are simulated.
128 devices in a mesh: pair: 8 (over x, core), ep: 16 (over z, y).
Axes of the slice: x: 4, y: 4, z: 4, core: 2. Of those that a mesh axis runs over, the one named last changes fastest.
Arguments:
- tokens: bfloat16 [32768, 4096], P(('pair', 'ep')), may hold values from -6 to 6
- expert_of: int32 [32768, 1], P(('pair', 'ep')), may hold values from 0 to 127, as said below
- w_gate: bfloat16 [128, 4096, 768], P(('pair', 'ep')), may hold values from -0.09375 to 0.09375
- w_up: bfloat16 [128, 4096, 768], P(('pair', 'ep')), may hold values from -0.09375 to 0.09375
- w_down: bfloat16 [128, 768, 4096], P(('pair', 'ep')), may hold values from -0.21875 to 0.21875
Outputs:
- mixed: bfloat16 [32768, 4096], P(('pair', 'ep'))
Inputs may be any that keep to these rules, and one draw needn't show every extreme that they name: `expert_of`: the rows of one device (aligned blocks of 256 tokens) name no expert more than 3 times; in every draw one expert, drawn from the seed, is named exactly 3 times in every device's rows.
All inputs are finite; a program needn't handle non-finite values.
Results may differ from a plain program's by a relative error of at most 0.005.
Values may be sent and summed in bfloat16 or wider, within the bound.
A program may use at most 128 MiB of HBM per device.

v0:
```python
import jax
import jax.numpy as jnp
from jax import lax
from jax.sharding import PartitionSpec as P


def shards(tokens, expert_of, w_gate, w_up, w_down):
    pair_count = lax.axis_size("pair")
    ep_count = lax.axis_size("ep")
    experts = pair_count * ep_count
    tok_rows = tokens.shape[0]
    capacity = tok_rows // experts + tok_rows // (2 * experts)
    routed = expert_of[:, 0]
    onehot = (routed[:, None] == jnp.arange(experts, dtype=jnp.int32)[None, :]).astype(jnp.float32)
    earlier_mask = (jnp.arange(tok_rows)[:, None] > jnp.arange(tok_rows)[None, :]).astype(
        jnp.float32
    )
    before = jnp.dot(earlier_mask, onehot, precision=lax.Precision.HIGHEST)
    slot_index = jnp.sum(before * onehot, axis=1).astype(jnp.int32)
    position = routed * capacity + slot_index
    outgoing = (
        jnp.zeros((experts * capacity, tokens.shape[1]), jnp.bfloat16).at[position].set(tokens)
    )
    parcel = lax.all_to_all(
        outgoing.reshape(experts, capacity, outgoing.shape[1]),
        ("pair", "ep"),
        split_axis=0,
        concat_axis=0,
        tiled=True,
    )
    senders = parcel.shape[0]
    per_sender = parcel.shape[1]
    flat_rows = parcel.reshape(senders * per_sender, parcel.shape[2])
    gate_proj = jnp.dot(flat_rows, w_gate[0], preferred_element_type=jnp.float32)
    up_proj = jnp.dot(flat_rows, w_up[0], preferred_element_type=jnp.float32)
    hidden = (jax.nn.silu(gate_proj) * up_proj).astype(jnp.bfloat16)
    result = jnp.dot(hidden, w_down[0], preferred_element_type=jnp.float32).astype(jnp.bfloat16)
    returned = lax.all_to_all(
        result.reshape(senders, per_sender, result.shape[1]),
        ("pair", "ep"),
        split_axis=0,
        concat_axis=0,
        tiled=True,
    )
    returned = returned.reshape(experts * capacity, returned.shape[2])
    return jnp.take(returned, position, axis=0)


def solution(mesh):
    in_specs = (
        P(("pair", "ep"), None),
        P(("pair", "ep"), None),
        P(("pair", "ep"), None, None),
        P(("pair", "ep"), None, None),
        P(("pair", "ep"), None, None),
    )
    out_specs = P(("pair", "ep"), None)
    return jax.shard_map(shards, mesh=mesh, in_specs=in_specs, out_specs=out_specs, check_vma=False)
```

profile of v0, /device:TPU:1, one launch (start us, length us, event | category | flops | bytes accessed | tf_op | source)
XLA Modules:
  0.0 176.6 jit_solution(17096203641321768983)
XLA Ops:
  0.0 1.0 fusion.17
  1.0 0.7 and_reduce_fusion
  1.7 5.5 %scatter_custom_fusion = bf16[384,4096]{1,0:T(8,128)(2,1)S(1)} fusion(s32[256]{0:T(256)S(1)} %bitcast.22, bf16[256,4096]{1,0:T(8,128)(2,1)} %param.5, bf16[]{:T(256)} %constant.25.clone.1), kind=kCustom, calls=%fused_computation.10 | custom fusion | bytes 3146240 | tf_op jit(solution)/shard_map/scatter | solution.py:22
  7.2 4.4 %reshape.25 = bf16[128,3,4096]{2,1,0:T(4,128)(2,1)} reshape(bf16[384,4096]{1,0:T(8,128)(2,1)S(1)} %scatter_custom_fusion) | data formatting | bytes 6291456 | tf_op jit(solution)/shard_map/reshape | solution.py:25
  11.6 62.7 %all_to_all.10 = bf16[128,3,4096]{2,1,0:T(4,128)(2,1)} all-to-all(bf16[128,3,4096]{2,1,0:T(4,128)(2,1)} %reshape.25), channel_id=1, replica_groups=mesh['pair'=8,'ep'=16] {'pair','ep'}, dimensions={0} | all-to-all | bytes 6291456 | tf_op jit(solution)/shard_map/all_to_all | solution.py:24
  74.3 6.0 %reshape.26 = bf16[384,4096]{1,0:T(8,128)(2,1)S(1)} reshape(bf16[128,3,4096]{2,1,0:T(4,128)(2,1)} %all_to_all.10) | data formatting | bytes 6291456 | tf_op jit(solution)/shard_map/reshape | solution.py:33
  80.3 6.4 %fusion.4 = f32[384,768]{1,0:T(8,128)} fusion(bf16[384,4096]{1,0:T(8,128)(2,1)S(1)} %reshape.26, bf16[1,4096,768]{2,1,0:T(8,128)(2,1)} %param.7), kind=kOutput, calls=%fused_computation.6 | convolution fusion | flops 2415919104 | bytes 10616832 | tf_op jit(solution)/shard_map/dot_general | solution.py:34
  86.7 13.3 %fusion.6 = bf16[384,4096]{1,0:T(8,128)(2,1)} fusion(bf16[1,768,4096]{2,1,0:T(8,128)(2,1)} %param.9, bf16[384,4096]{1,0:T(8,128)(2,1)S(1)} %reshape.26, bf16[1,4096,768]{2,1,0:T(8,128)(2,1)} %param.8, f32[384,768]{1,0:T(8,128)} %fusion.4), kind=kOutput, calls=%fused_computation.8 | convolution fusion | flops 4835180544 | bytes 20054016 | tf_op jit(solution)/shard_map/dot_general | solution.py:37
  100.0 7.1 %reshape.27 = bf16[128,3,4096]{2,1,0:T(4,128)(2,1)} reshape(bf16[384,4096]{1,0:T(8,128)(2,1)} %fusion.6) | data formatting | bytes 6291456 | tf_op jit(solution)/shard_map/reshape | solution.py:39
  107.0 6.4 %all-to-all-start.1 = ((bf16[128,3,4096]{2,1,0:T(4,128)(2,1)}), bf16[128,3,4096]{2,1,0:T(4,128)(2,1)}, u32[]{:S(2)}, u32[]{:S(2)}) async-start(bf16[128,3,4096]{2,1,0:T(4,128)(2,1)} %reshape.27), calls=%async_computation.1 | async-start | bytes 8388608 | tf_op jit(solution)/shard_map/all_to_all | solution.py:38
  113.5 50.8 %all-to-all-done.1 = bf16[128,3,4096]{2,1,0:T(4,128)(2,1)} async-done(((bf16[128,3,4096]{2,1,0:T(4,128)(2,1)}), bf16[128,3,4096]{2,1,0:T(4,128)(2,1)}, u32[]{:S(2)}, u32[]{:S(2)}) %all-to-all-start.1) | async-done | bytes 3145760 | tf_op jit(solution)/shard_map/all_to_all | solution.py:38
  164.3 6.0 %reshape.28 = bf16[384,4096]{1,0:T(8,128)(2,1)S(1)} reshape(bf16[128,3,4096]{2,1,0:T(4,128)(2,1)} %all-to-all-done.1) | data formatting | bytes 6291456 | tf_op jit(solution)/shard_map/reshape | solution.py:45
  170.3 3.2 %gather_fusion = bf16[256,4096]{1,0:T(8,128)(2,1)} fusion(bf16[384,4096]{1,0:T(8,128)(2,1)S(1)} %reshape.28, s32[1024]{0:T(1024)S(1)} %pad_clamp_fusion), kind=kCustom, calls=%fused_computation | custom fusion | bytes 4195328 | tf_op jit(solution)/shard_map/jit(_take)/gather | solution.py:46
  173.4 3.2 %broadcast_select_fusion = bf16[256,4096]{1,0:T(8,128)(2,1)} fusion(bf16[256,4096]{1,0:T(8,128)(2,1)} %gather_fusion, pred[256]{0:T(512)(128)(4,1)S(1)} %get-tuple-element.5), kind=kLoop, calls=%fused_computation.9 | loop fusion | flops 1048576 | bytes 4194560 | tf_op jit(solution)/shard_map/jit(_take)/select_n | solution.py:46
  (2 shorter events, 0.0 us)
Async XLA Ops:
  107.0 57.3 %all-to-all-start.1 = ((bf16[128,3,4096]{2,1,0:T(4,128)(2,1)}), bf16[128,3,4096]{2,1,0:T(4,128)(2,1)}, u32[]{:S(2)}, u32[]{:S(2)}) async-start(bf16[128,3,4096]{2,1,0:T(4,128)(2,1)} %reshape.27), calls=%async_computation.1 | async-start | bytes 8388608 | tf_op jit(solution)/shard_map/all_to_all | solution.py:38
where the time goes:
time: 178 us; the launch traced here: 177 us
  blocking collectives  62.7 us (35%)
  waiting for transfers between devices  50.8 us (29%)
  local copies, waits for them, and re-layouts  32.1 us (18%)
  matrix products  20.7 us (12%)
  starting transfers between devices  6.41 us (4%)
  other arithmetic  3.88 us (2%)
    all_to_all x1, blocking collectives, shards(): lax.all_to_all(outgoing.reshape(experts, capacity, outgoing.shape[1]), ('...  62.7 us
    all_to_all x1, waiting for transfers between devices, shards(): lax.all_to_all(result.reshape(senders, per_sender, result.shape[1]), ('pa...  50.8 us
    dot_general x1, matrix products, shards(): jnp.dot(hidden, w_down[0], preferred_element_type=jnp.float32)  13.3 us
    reshape x1, local copies, waits for them, and re-layouts, shards(): result.reshape(senders, per_sender, result.shape[1])  7.08 us
    all_to_all x1, starting transfers between devices, shards(): lax.all_to_all(result.reshape(senders, per_sender, result.shape[1]), ('pa...  6.41 us
    dot_general x1, matrix products, shards(): jnp.dot(flat_rows, w_gate[0], preferred_element_type=jnp.float32)  6.39 us
    reshape x1, local copies, waits for them, and re-layouts, shards(): flat_rows = parcel.reshape(senders * per_sender, parcel.shape[2])  5.96 us
    reshape x1, local copies, waits for them, and re-layouts, shards(): returned = returned.reshape(experts * capacity, returned.shape[2])  5.96 us
  transfers between devices with their start and end apart: 1, of which 1 were waited for; matrix products, arithmetic and copies ran while one was open for 0% of the time, Pallas kernels for 0%

commit v1 on v0

v1 whole, which is shorter than its diff:
```python
import functools

import jax
import jax.numpy as jnp
from jax import lax
from jax.experimental import pallas as pl
from jax.experimental.pallas import tpu as pltpu
from jax.sharding import PartitionSpec as P

MESH = pl.DeviceIdType.MESH
BF16 = jnp.bfloat16
F32 = jnp.float32

DEVICES = 128
CAP = 3
STEP = 37
UNSTEP = pow(STEP, -1, DEVICES)
CUT, WIDE = 16, 256
GROUPS = ((0, 64), (64, 64))


def dims():
    pair, ep = lax.axis_index("pair"), lax.axis_index("ep")
    return pair // 2, pair % 2, ep // 4, ep % 4


def peer(step, sign):
    off = (step * STEP) % DEVICES
    x, core, z, y = dims()
    px = (x + 4 + sign * (off // 32)) % 4
    pc = (core + off // 16) % 2
    pz = (z + 4 + sign * ((off // 4) % 4)) % 4
    py = (y + 4 + sign * (off % 4)) % 4
    return px * 2 + pc, pz * 4 + py


def step_of(expert):
    x, core, z, y = dims()
    dx = (expert // 32 + 4 - x) % 4
    dc = ((expert // 16) % 2 + core) % 2
    dz = ((expert // 4) % 4 + 4 - z) % 4
    dy = (expert % 4 + 4 - y) % 4
    return ((dx * 32 + dc * 16 + dz * 4 + dy) * UNSTEP) % DEVICES


def kernel(
    expert_ref, tok_hbm, wg_hbm, wu_hbm, wd_hbm, mixed_ref,
    tok, wg, wu, wd, rows, hid, pick, place, turn, outgoing, parcel, result, returned,
    tok_sem, w_sem, send_sem, there_sem, back_send_sem, back_sem,
):
    barrier = pltpu.get_barrier_semaphore()

    @pl.loop(1, DEVICES)
    def _(k):
        pl.semaphore_signal(barrier, inc=1, device_id=peer(k, 1), device_id_type=MESH)

    tok_copy = pltpu.make_async_copy(tok_hbm, tok, tok_sem)
    tok_copy.start()
    w_copies = [
        pltpu.make_async_copy(src.at[0], dst, w_sem.at[i])
        for i, (src, dst) in enumerate(((wg_hbm, wg), (wu_hbm, wu), (wd_hbm, wd)))
    ]
    for copy in w_copies:
        copy.start()

    count = tok.shape[0]
    slots = DEVICES * CAP
    column = expert_ref[...]
    down = lax.broadcasted_iota(jnp.int32, (count, count), 0)
    across = lax.broadcasted_iota(jnp.int32, (count, count), 1)
    row = jnp.sum(jnp.where(down == across, column, 0), axis=0, keepdims=True)
    same = column == row
    row_rank = jnp.sum(jnp.where(same & (down < across), 1, 0), axis=0, keepdims=True)
    col_rank = jnp.sum(jnp.where(same & (across < down), 1, 0), axis=1, keepdims=True)
    row_slot = step_of(row) * CAP + row_rank
    col_slot = step_of(column) * CAP + col_rank
    pick[...] = jnp.where(
        lax.broadcasted_iota(jnp.int32, (slots, count), 0) == row_slot, 1.0, 0.0
    ).astype(BF16)
    place[...] = jnp.where(
        lax.broadcasted_iota(jnp.int32, (count, slots), 1) == col_slot, 1.0, 0.0
    ).astype(BF16)
    n = CUT * CUT
    turn_row = lax.broadcasted_iota(jnp.int32, (n, n), 0)
    turn_col = lax.broadcasted_iota(jnp.int32, (n, n), 1)
    turn[...] = jnp.where(
        (turn_row // CUT == turn_col % CUT) & (turn_row % CUT == turn_col // CUT), 1.0, 0.0
    ).astype(BF16)

    def pack(src, dst, block):
        at = pl.multiple_of(block * CUT, CUT)
        cut = jnp.concatenate(
            [src[pl.ds(at, CUT), c * WIDE : (c + 1) * WIDE] for c in range(CUT)], axis=0
        )
        turned = jnp.dot(turn[...], cut, preferred_element_type=F32).astype(BF16)
        dst[pl.ds(pl.multiple_of(block * n, n), n), :] = turned

    def unpack(src, dst, block):
        at = pl.multiple_of(block * CUT, CUT)
        cut = src[pl.ds(pl.multiple_of(block * n, n), n), :]
        turned = jnp.dot(turn[...], cut, preferred_element_type=F32).astype(BF16)
        for c in range(CUT):
            dst[pl.ds(at, CUT), c * WIDE : (c + 1) * WIDE] = turned[c * CUT : (c + 1) * CUT, :]

    parcel_rows = CAP * CUT

    def span(step, steps=1):
        return pl.ds(pl.multiple_of(step * parcel_rows, parcel_rows), steps * parcel_rows)

    def there(k, sem):
        return pltpu.make_async_remote_copy(
            src_ref=outgoing.at[span(k)], dst_ref=parcel.at[span(k)],
            send_sem=send_sem, recv_sem=sem, device_id=peer(k, 1), device_id_type=MESH,
        )

    def back(k, sem):
        return pltpu.make_async_remote_copy(
            src_ref=result.at[span(k)], dst_ref=returned.at[span(k)],
            send_sem=back_send_sem, recv_sem=sem, device_id=peer(k, -1), device_id_type=MESH,
        )

    tok_copy.wait()

    @pl.loop(0, CUT)
    def _(c):
        at = pl.ds(pl.multiple_of(c * WIDE, WIDE), WIDE)
        rows[:, at] = jnp.dot(pick[...], tok[:, at], preferred_element_type=F32).astype(BF16)

    unit = 16
    blocks = unit * CAP // CUT
    units = DEVICES // unit

    def pack_unit(u):
        @pl.loop(0, blocks)
        def _(b):
            pack(rows, outgoing, u * blocks + b)

    for g, (first, steps) in enumerate(GROUPS):
        for u in range(first // unit, (first + steps) // unit):
            if u == 0:
                pack_unit(0)
                pl.semaphore_wait(barrier, DEVICES - 1)
            if u + 1 < units:
                pack_unit(u + 1)

            @pl.loop(max(u * unit, 1), (u + 1) * unit)
            def _(k):
                there(k, there_sem.at[g]).start()

    parcel[: parcel_rows, :] = outgoing[: parcel_rows, :]

    for g, (first, steps) in enumerate(GROUPS):
        lo = max(first, 1)
        got = span(lo, first + steps - lo)
        pltpu.make_async_remote_copy(
            src_ref=outgoing.at[got], dst_ref=parcel.at[got], send_sem=send_sem,
            recv_sem=there_sem.at[g], device_id=peer(1, 1), device_id_type=MESH,
        ).wait_recv()
        r0, m = first * CAP, steps * CAP

        @pl.loop(r0 // CUT, (r0 + m) // CUT)
        def _(b):
            unpack(parcel, rows, b)

        if g == 0:
            w_copies[0].wait()
            w_copies[1].wait()

        @pl.loop(0, wg.shape[1] // WIDE)
        def _(j):
            at = pl.ds(pl.multiple_of(j * WIDE, WIDE), WIDE)
            x = rows[r0 : r0 + m, :]
            gate = jnp.dot(x, wg[:, at], preferred_element_type=F32)
            up = jnp.dot(x, wu[:, at], preferred_element_type=F32)
            hid[:m, at] = (gate / (1.0 + jnp.exp(-gate)) * up).astype(BF16)

        if g == 0:
            w_copies[2].wait()

        @pl.loop(0, CUT)
        def _(c):
            at = pl.ds(pl.multiple_of(c * WIDE, WIDE), WIDE)
            rows[r0 : r0 + m, at] = jnp.dot(
                hid[:m, :], wd[:, at], preferred_element_type=F32
            ).astype(BF16)

        @pl.loop(r0 // CUT, (r0 + m) // CUT)
        def _(b):
            pack(rows, result, b)

        @pl.loop(lo, first + steps)
        def _(k):
            back(k, back_sem.at[g]).start()

        if g == 0:
            returned[: parcel_rows, :] = result[: parcel_rows, :]

    for g, (first, steps) in enumerate(GROUPS):
        lo = max(first, 1)
        got = span(lo, first + steps - lo)
        pltpu.make_async_remote_copy(
            src_ref=result.at[got], dst_ref=returned.at[got], send_sem=back_send_sem,
            recv_sem=back_sem.at[g], device_id=peer(1, 1), device_id_type=MESH,
        ).wait_recv()

        @pl.loop(first * CAP // CUT, (first + steps) * CAP // CUT)
        def _(b):
            unpack(returned, rows, b)

    @pl.loop(0, CUT)
    def _(c):
        at = pl.ds(pl.multiple_of(c * WIDE, WIDE), WIDE)
        mixed_ref[:, at] = jnp.dot(
            place[...], rows[:, at], preferred_element_type=F32
        ).astype(BF16)

    sent = span(1, DEVICES - 1)
    for src, dst, sem in ((outgoing, parcel, send_sem), (result, returned, back_send_sem)):
        pltpu.make_async_remote_copy(
            src_ref=src.at[sent], dst_ref=dst.at[sent], send_sem=sem,
            recv_sem=there_sem.at[0], device_id=peer(1, 1), device_id_type=MESH,
        ).wait_send()


def shards(tokens, expert_of, w_gate, w_up, w_down):
    count, width = tokens.shape
    hidden = w_gate.shape[2]
    slots = DEVICES * CAP
    packed = pltpu.VMEM((slots * CUT, WIDE), BF16)
    hbm = pl.BlockSpec(memory_space=pl.ANY)
    vmem = pl.BlockSpec(memory_space=pltpu.VMEM)
    return pl.pallas_call(
        kernel,
        out_shape=jax.ShapeDtypeStruct((count, width), BF16),
        in_specs=[vmem, hbm, hbm, hbm, hbm],
        out_specs=vmem,
        scratch_shapes=[
            pltpu.VMEM((count, width), BF16),
            pltpu.VMEM((width, hidden), BF16),
            pltpu.VMEM((width, hidden), BF16),
            pltpu.VMEM((hidden, width), BF16),
            pltpu.VMEM((slots, width), BF16),
            pltpu.VMEM((max(s for _, s in GROUPS) * CAP, hidden), BF16),
            pltpu.VMEM((slots, count), BF16),
            pltpu.VMEM((count, slots), BF16),
            pltpu.VMEM((CUT * CUT, CUT * CUT), BF16),
            packed, packed, packed, packed,
            pltpu.SemaphoreType.DMA,
            pltpu.SemaphoreType.DMA((3,)),
            pltpu.SemaphoreType.DMA,
            pltpu.SemaphoreType.DMA((len(GROUPS),)),
            pltpu.SemaphoreType.DMA,
            pltpu.SemaphoreType.DMA((len(GROUPS),)),
        ],
        compiler_params=pltpu.CompilerParams(
            collective_id=0, has_side_effects=True, vmem_limit_bytes=56 * 1024 * 1024
        ),
        name="expert_exchange",
    )(expert_of, tokens, w_gate, w_up, w_down)


def solution(mesh):
    rows = P(("pair", "ep"), None)
    blocks = P(("pair", "ep"), None, None)
    return jax.shard_map(
        shards, mesh=mesh, in_specs=(rows, rows, blocks, blocks, blocks), out_specs=rows,
        check_vma=False,
    )
```

time: 178 us -> 114 us (0.64)
  the two profiles are of different devices: /device:TPU:1 before, /device:TPU:65 now
where the time goes in v1:
time: 114 us
  Pallas kernels  109 us (96%)
  local copies, waits for them, and re-layouts  4.6 us (4%)
    pallas_call x1, Pallas kernels, shards(): pl.pallas_call(kernel, out_shape=jax.ShapeDtypeStruct((count, width), BF1...  109 us
    unnamed x2, local copies, waits for them, and re-layouts  4.6 us

profile of v1, /device:TPU:65, one launch (start us, length us, event | category | flops | bytes accessed | tf_op | source)
XLA Modules:
  0.0 114.1 jit_solution(9543545935023519548)
XLA Ops:
  0.0 1.5 %copy.6.expert_ref = s32[256,1]{1,0:T(8,128)} copy(s32[256,1]{0,1:T(1,128)} %param.6) | data formatting | bytes 2048 | tf_op args[1]
  1.5 109.5 %expert_exchange.1 = bf16[256,4096]{1,0:T(8,128)(2,1)} custom-call(s32[256,1]{1,0:T(8,128)} %copy.6.expert_ref, bf16[256,4096]{1,0:T(8,128)(2,1)} %tok_hbm.1, bf16[1,4096,768]{2,1,0:T(8,128)(2,1)} %wg_hbm.1, bf16[1,4096,768]{2,1,0:T(8,128)(2,1)} %wu_hbm.1, bf16[1,768,4096]{2,1,0:T(8,128)(2,1)} %wd_hbm.1), custom_call_target="tpu_custom_call" | custom-call | tf_op jit(solution)/shard_map/expert_exchange/pallas_call | solution.py:232
  111.0 3.1 %copy.8 = bf16[256,4096]{1,0:T(8,128)(2,1)} copy(bf16[256,4096]{1,0:T(8,128)(2,1)} %expert_exchange.1) | data formatting | bytes 4194304

commit v2 on v0

v2 whole, which is shorter than its diff:
```python
import jax
import jax.numpy as jnp
from jax import lax
from jax.experimental import pallas as pl
from jax.experimental.pallas import tpu as pltpu
from jax.sharding import PartitionSpec as P

MESH = pl.DeviceIdType.MESH
BF16 = jnp.bfloat16
F32 = jnp.float32

DEVICES = 128
CAP = 3
STEP = 37
UNSTEP = pow(STEP, -1, DEVICES)
CUT, WIDE = 16, 256
UNIT = 32
SLOTS = UNIT * CAP
BLOCKS = SLOTS // CUT
UNITS = DEVICES // UNIT
GROUPS = ((0, 1), (2, 3))
LANDINGS = ((0, 1), (2,), (3,))
SPREAD = 1024


def step_of(expert, x, core, z, y):
    dx = (expert // 32 + 4 - x) % 4
    dc = ((expert // 16) % 2 + core) % 2
    dz = ((expert // 4) % 4 + 4 - z) % 4
    dy = (expert % 4 + 4 - y) % 4
    return ((dx * 32 + dc * 16 + dz * 4 + dy) * UNSTEP) % DEVICES


def kernel(
    expert_hbm, tok_hbm, wg_hbm, wu_hbm, wd_hbm, mixed_ref,
    expert, tok, wg, wu, wd, rows, hid, place, turn, outgoing, parcel, result, returned,
    expert_sem, tok_sem, w_sem, send_sem, there_sem, back_send_sem, back_sem,
):
    pair, ep = lax.axis_index("pair"), lax.axis_index("ep")
    x, core, z, y = pair // 2, pair % 2, ep // 4, ep % 4
    pairs = [((x + d // 2) % 4) * 2 + (core + d % 2) % 2 for d in range(8)]
    eps = [((z + d // 4) % 4) * 4 + (y + d % 4) % 4 for d in range(16)]

    def peer(step, sign):
        off = (step * STEP) % DEVICES
        dx, dc, dz, dy = off // 32, (off // 16) % 2, (off // 4) % 4, off % 4
        return pairs[(sign * dx) % 4 * 2 + dc], eps[(sign * dz) % 4 * 4 + (sign * dy) % 4]

    expert_copy = pltpu.make_async_copy(expert_hbm, expert, expert_sem)
    expert_copy.start()
    tok_copy = pltpu.make_async_copy(tok_hbm, tok, tok_sem)
    tok_copy.start()
    barrier = pltpu.get_barrier_semaphore()
    for k in range(1, DEVICES):
        pl.semaphore_signal(barrier, inc=1, device_id=peer(k, 1), device_id_type=MESH)

    count = tok.shape[0]
    expert_copy.wait()
    row = expert[...]
    down = lax.broadcasted_iota(jnp.int32, (count, count), 0)
    across = lax.broadcasted_iota(jnp.int32, (count, count), 1)
    column = jnp.sum(jnp.where(down == across, row, 0), axis=1, keepdims=True)
    same = column == row
    row_rank = jnp.sum(jnp.where(same & (down < across), 1, 0), axis=0, keepdims=True)
    row_slot = step_of(row, x, core, z, y) * CAP + row_rank
    n = CUT * CUT
    turn_row = lax.broadcasted_iota(jnp.int32, (n, n), 0)
    turn_col = lax.broadcasted_iota(jnp.int32, (n, n), 1)
    turn[...] = jnp.where(
        (turn_row // CUT == turn_col % CUT) & (turn_row % CUT == turn_col // CUT), 1.0, 0.0
    ).astype(BF16)

    def pack(src, dst, unit):
        for b in range(unit * BLOCKS, (unit + 1) * BLOCKS):
            cut = jnp.concatenate(
                [src[b * CUT : (b + 1) * CUT, c * WIDE : (c + 1) * WIDE] for c in range(CUT)],
                axis=0,
            )
            turned = jnp.dot(turn[...], cut, preferred_element_type=F32).astype(BF16)
            dst[b * n : (b + 1) * n, :] = turned

    def unpack(src, dst, unit):
        for b in range(unit * BLOCKS, (unit + 1) * BLOCKS):
            cut = src[b * n : (b + 1) * n, :]
            turned = jnp.dot(turn[...], cut, preferred_element_type=F32).astype(BF16)
            for c in range(CUT):
                dst[b * CUT : (b + 1) * CUT, c * WIDE : (c + 1) * WIDE] = turned[
                    c * CUT : (c + 1) * CUT, :
                ]

    def spread(body):
        @pl.loop(0, tok.shape[1] // SPREAD)
        def _(c):
            body(pl.ds(pl.multiple_of(c * SPREAD, SPREAD), SPREAD))

    parcel_rows = CAP * CUT

    def span(step, steps=1):
        return pl.ds(step * parcel_rows, steps * parcel_rows)

    def there(k, steps=1):
        return pltpu.make_async_remote_copy(
            src_ref=outgoing.at[span(k, steps)], dst_ref=parcel.at[span(k, steps)],
            send_sem=send_sem, recv_sem=there_sem.at[[k // UNIT in g for g in GROUPS].index(True)],
            device_id=peer(k, 1), device_id_type=MESH,
        )

    def back(k, steps=1):
        return pltpu.make_async_remote_copy(
            src_ref=result.at[span(k, steps)], dst_ref=returned.at[span(k, steps)],
            send_sem=back_send_sem,
            recv_sem=back_sem.at[[k // UNIT in g for g in LANDINGS].index(True)],
            device_id=peer(k, -1), device_id_type=MESH,
        )

    def send(copy, unit):
        for k in range(max(unit * UNIT, 1), (unit + 1) * UNIT):
            copy(k).start()

    def await_units(copy, units):
        lo = max(units[0] * UNIT, 1)
        copy(lo, (units[-1] + 1) * UNIT - lo).wait_recv()

    def select(unit):
        pick = jnp.where(
            lax.broadcasted_iota(jnp.int32, (SLOTS, count), 0) + unit * SLOTS == row_slot, 1.0, 0.0
        ).astype(BF16)

        @spread
        def _(at):
            rows[unit * SLOTS : (unit + 1) * SLOTS, at] = jnp.dot(
                pick, tok[:, at], preferred_element_type=F32
            ).astype(BF16)

    tok_copy.wait()
    for u in range(UNITS):
        select(u)
        pack(rows, outgoing, u)
        if u == 0:
            pl.semaphore_wait(barrier, DEVICES - 1)
        else:
            send(there, u - 1)
    send(there, UNITS - 1)
    parcel[:parcel_rows, :] = outgoing[:parcel_rows, :]

    w_copies = [
        pltpu.make_async_copy(src.at[0], dst, w_sem.at[i])
        for i, (src, dst) in enumerate(((wg_hbm, wg), (wu_hbm, wu), (wd_hbm, wd)))
    ]
    for copy in w_copies:
        copy.start()

    col_rank = jnp.sum(jnp.where(same & (across < down), 1, 0), axis=1, keepdims=True)
    col_slot = step_of(column, x, core, z, y) * CAP + col_rank
    place[...] = jnp.where(
        lax.broadcasted_iota(jnp.int32, (count, DEVICES * CAP), 1) == col_slot, 1.0, 0.0
    ).astype(BF16)
    for copy in w_copies:
        copy.wait()

    for units in GROUPS:
        await_units(there, units)
        for u in units:
            unpack(parcel, rows, u)
        held = slice(units[0] * SLOTS, (units[-1] + 1) * SLOTS)
        for j in range(0, wg.shape[1], WIDE):
            arrived = rows[held, :]
            gate = jnp.dot(arrived, wg[:, j : j + WIDE], preferred_element_type=F32)
            up = jnp.dot(arrived, wu[:, j : j + WIDE], preferred_element_type=F32)
            hid[held, j : j + WIDE] = (gate / (1.0 + jnp.exp(-gate)) * up).astype(BF16)

        @spread
        def _(at):
            rows[held, at] = jnp.dot(hid[held, :], wd[:, at], preferred_element_type=F32).astype(BF16)

        for i, u in enumerate(units):
            pack(rows, result, u)
            if i:
                send(back, units[i - 1])
        send(back, units[-1])
        if units[0] == 0:
            returned[:parcel_rows, :] = result[:parcel_rows, :]

    for units in LANDINGS:
        await_units(back, units)
        for u in units:
            unpack(returned, rows, u)
        if units == LANDINGS[0]:
            early = (units[-1] + 1) * SLOTS

            @spread
            def _(at):
                mixed_ref[:, at] = jnp.dot(
                    place[:, :early], rows[:early, at], preferred_element_type=F32
                ).astype(BF16)

    @spread
    def _(at):
        late = jnp.dot(place[:, early:], rows[early:, at], preferred_element_type=F32)
        mixed_ref[:, at] = (mixed_ref[:, at].astype(F32) + late).astype(BF16)

    there(1, DEVICES - 1).wait_send()
    back(1, DEVICES - 1).wait_send()


def shards(tokens, expert_of, w_gate, w_up, w_down):
    count, width = tokens.shape
    hidden = w_gate.shape[2]
    slots = DEVICES * CAP
    packed = pltpu.VMEM((slots * CUT, WIDE), BF16)
    hbm = pl.BlockSpec(memory_space=pltpu.HBM)
    vmem = pl.BlockSpec(memory_space=pltpu.VMEM)
    return pl.pallas_call(
        kernel,
        out_shape=jax.ShapeDtypeStruct((count, width), BF16),
        in_specs=[hbm, hbm, hbm, hbm, hbm],
        out_specs=vmem,
        scratch_shapes=[
            pltpu.VMEM((1, count), jnp.int32),
            pltpu.VMEM((count, width), BF16),
            pltpu.VMEM((width, hidden), BF16),
            pltpu.VMEM((width, hidden), BF16),
            pltpu.VMEM((hidden, width), BF16),
            pltpu.VMEM((slots, width), BF16),
            pltpu.VMEM((slots, hidden), BF16),
            pltpu.VMEM((count, slots), BF16),
            pltpu.VMEM((CUT * CUT, CUT * CUT), BF16),
            packed, packed, packed, packed,
            pltpu.SemaphoreType.DMA,
            pltpu.SemaphoreType.DMA,
            pltpu.SemaphoreType.DMA((3,)),
            pltpu.SemaphoreType.DMA,
            pltpu.SemaphoreType.DMA((len(GROUPS),)),
            pltpu.SemaphoreType.DMA,
            pltpu.SemaphoreType.DMA((len(LANDINGS),)),
        ],
        compiler_params=pltpu.CompilerParams(
            collective_id=0, has_side_effects=True, vmem_limit_bytes=50 * 1024 * 1024
        ),
        name="expert_exchange",
    )(expert_of.reshape(1, count), tokens, w_gate, w_up, w_down)


def solution(mesh):
    rows = P(("pair", "ep"), None)
    blocks = P(("pair", "ep"), None, None)
    return jax.shard_map(
        shards, mesh=mesh, in_specs=(rows, rows, blocks, blocks, blocks), out_specs=rows,
        check_vma=False,
    )
```

time: 178 us -> 88.6 us (0.50)
  Pallas kernels: 0 us -> 85.1 us
  blocking collectives: 62.7 us -> 0 us
  waiting for transfers between devices: 50.8 us -> 0 us
  local copies, waits for them, and re-layouts: 32.1 us -> 2 us
  matrix products: 20.7 us -> 0 us
  starting transfers between devices: 6.41 us -> 0 us
  other arithmetic: 3.88 us -> 0 us
    pallas_call x0 -> x1, Pallas kernels: none -> 85.1 us  [shards(): pl.pallas_call(kernel, out_shape=jax.ShapeDtypeStruct((count, width), BF1...]
    all_to_all x1 -> x0, blocking collectives: 62.7 us -> none  [shards(): lax.all_to_all(outgoing.reshape(experts, capacity, outgoing.shape[1]), ('...]
    all_to_all x1 -> x0, waiting for transfers between devices: 50.8 us -> none  [shards(): lax.all_to_all(result.reshape(senders, per_sender, result.shape[1]), ('pa...]
    reshape x4 -> x0, local copies, waits for them, and re-layouts: 23.5 us -> none  [the longest x1 7.08 us: shards(): result.reshape(senders, per_sender, result.shape[1])]
    dot_general x3 -> x0, matrix products: 20.7 us -> none  [the longest x1 13.3 us: shards(): jnp.dot(hidden, w_down[0], preferred_element_type=jnp.float32)]
    all_to_all x1 -> x0, starting transfers between devices: 6.41 us -> none  [shards(): lax.all_to_all(result.reshape(senders, per_sender, result.shape[1]), ('pa...]
    scatter x1 -> x0, local copies, waits for them, and re-layouts: 5.48 us -> none  [shards(): jnp.zeros((experts * capacity, tokens.shape[1]), jnp.bfloat16).at[position]]
    gather x1 -> x0, local copies, waits for them, and re-layouts: 3.17 us -> none  [shards(): return jnp.take(returned, position, axis=0)]
  transfers between devices with their start and end apart: 1 -> 0, of which waited for: 1 -> 0; matrix products, arithmetic and copies ran while one was open for 0% -> 0% of each run, Pallas kernels for 0% -> 0%
where the time goes in v2:
time: 88.6 us; the launch traced here: 87.1 us
  Pallas kernels  85.1 us (96%)
  local copies, waits for them, and re-layouts  2 us (2%)
    pallas_call x1, Pallas kernels, shards(): pl.pallas_call(kernel, out_shape=jax.ShapeDtypeStruct((count, width), BF1...  85.1 us
    unnamed x3, local copies, waits for them, and re-layouts  2 us

profile of v2, /device:TPU:1, one launch (start us, length us, event | category | flops | bytes accessed | tf_op | source)
XLA Modules:
  0.0 87.1 jit_solution(17949551013339612121)
XLA Ops:
  0.0 0.0 copy-start
  0.0 0.7 copy-done
  0.7 85.1 %expert_exchange.1 = bf16[256,4096]{1,0:T(8,128)(2,1)S(1)} custom-call(s32[1,256]{1,0:T(1,128)S(1)} %bitcast.1, bf16[256,4096]{1,0:T(8,128)(2,1)} %tok_hbm.1, bf16[1,4096,768]{2,1,0:T(8,128)(2,1)} %wg_hbm.1, bf16[1,4096,768]{2,1,0:T(8,128)(2,1)} %wu_hbm.1, bf16[1,768,4096]{2,1,0:T(8,128)(2,1)} %wd_hbm.1), custom_call_target="tpu_custom_call" | custom-call | tf_op jit(solution)/shard_map/expert_exchange/pallas_call | solution.py:213
  85.8 1.3 %copy.7 = bf16[256,4096]{1,0:T(8,128)(2,1)} copy(bf16[256,4096]{1,0:T(8,128)(2,1)S(1)} %expert_exchange.1) | data formatting | bytes 4194304
Async XLA Ops:
  0.0 0.7 copy-start

commit v3 on v2

--- a/solution.py
+++ b/solution.py
@@ -1,3 +1,5 @@
+import random
+
 import jax
 import jax.numpy as jnp
 from jax import lax
@@ -11,16 +13,47 @@
 
 DEVICES = 128
 CAP = 3
-STEP = 37
-UNSTEP = pow(STEP, -1, DEVICES)
 CUT, WIDE = 16, 256
-UNIT = 32
+UNIT = 16
 SLOTS = UNIT * CAP
 BLOCKS = SLOTS // CUT
 UNITS = DEVICES // UNIT
-GROUPS = ((0, 1), (2, 3))
-LANDINGS = ((0, 1), (2,), (3,))
+GROUPS = ((0, 1, 2, 3), (4, 5, 6, 7))
+LANDINGS = ((0, 1, 2, 3), (4, 5, 6), (7,))
+AHEAD = 3
 SPREAD = 1024
+
+
+def split(off):
+    return off // 32, (off // 16) % 2, (off // 4) % 4, off % 4
+
+
+def distance(off):
+    dx, _, dz, dy = split(off)
+    return sum(min(d, 4 - d) for d in (dx, dz, dy))
+
+
+def even_order():
+    def hops(off):
+        dx, _, dz, dy = split(off)
+        return [int(d in way) for d in (dx, dz, dy) for way in ((1, 2), (3, 2))]
+
+    def spread_of(off):
+        total = [a + b for a, b in zip(load, hops(off))]
+        return sum(t * t for t in total) * len(total) - sum(total) ** 2
+
+    rng = random.Random(1)
+    rest, load, order = list(range(1, DEVICES)), [0] * 6, [0]
+    while rest:
+        rng.shuffle(rest)
+        best = min(rest, key=spread_of)
+        rest.remove(best)
+        load = [a + b for a, b in zip(load, hops(best))]
+        order.append(best)
+    return order
+
+
+ORDER = even_order()
 
 
 def step_of(expert, x, core, z, y):
@@ -28,7 +61,11 @@
     dc = ((expert // 16) % 2 + core) % 2
     dz = ((expert // 4) % 4 + 4 - z) % 4
     dy = (expert % 4 + 4 - y) % 4
-    return ((dx * 32 + dc * 16 + dz * 4 + dy) * UNSTEP) % DEVICES
+    off = dx * 32 + dc * 16 + dz * 4 + dy
+    step = jnp.zeros_like(off)
+    for k, met in enumerate(ORDER):
+        step = jnp.where(off == met, k, step)
+    return step
 
 
 def kernel(
@@ -42,8 +79,7 @@
     eps = [((z + d // 4) % 4) * 4 + (y + d % 4) % 4 for d in range(16)]
 
     def peer(step, sign):
-        off = (step * STEP) % DEVICES
-        dx, dc, dz, dy = off // 32, (off // 16) % 2, (off // 4) % 4, off % 4
+        dx, dc, dz, dy = split(ORDER[step])
         return pairs[(sign * dx) % 4 * 2 + dc], eps[(sign * dz) % 4 * 4 + (sign * dy) % 4]
 
     expert_copy = pltpu.make_async_copy(expert_hbm, expert, expert_sem)
@@ -51,7 +87,7 @@
     tok_copy = pltpu.make_async_copy(tok_hbm, tok, tok_sem)
     tok_copy.start()
     barrier = pltpu.get_barrier_semaphore()
-    for k in range(1, DEVICES):
+    for k in sorted(range(1, DEVICES), key=lambda k: -distance(ORDER[k])):
         pl.semaphore_signal(barrier, inc=1, device_id=peer(k, 1), device_id_type=MESH)
 
     count = tok.shape[0]
@@ -136,9 +172,11 @@
     for u in range(UNITS):
         select(u)
         pack(rows, outgoing, u)
-        if u == 0:
+        if u == AHEAD - 1:
             pl.semaphore_wait(barrier, DEVICES - 1)
-        else:
+            for v in range(AHEAD - 1):
+                send(there, v)
+        if u >= AHEAD:
             send(there, u - 1)
     send(there, UNITS - 1)
     parcel[:parcel_rows, :] = outgoing[:parcel_rows, :]
@@ -150,8 +188,7 @@
     for copy in w_copies:
         copy.start()
 
-    col_rank = jnp.sum(jnp.where(same & (across < down), 1, 0), axis=1, keepdims=True)
-    col_slot = step_of(column, x, core, z, y) * CAP + col_rank
+    col_slot = jnp.sum(jnp.where(down == across, row_slot, 0), axis=1, keepdims=True)
     place[...] = jnp.where(
         lax.broadcasted_iota(jnp.int32, (count, DEVICES * CAP), 1) == col_slot, 1.0, 0.0
     ).astype(BF16)
@@ -185,7 +222,7 @@
         await_units(back, units)
         for u in units:
             unpack(returned, rows, u)
-        if units == LANDINGS[0]:
+        if units == LANDINGS[-2]:
             early = (units[-1] + 1) * SLOTS
 
             @spread
@@ -238,7 +275,7 @@
             collective_id=0, has_side_effects=True, vmem_limit_bytes=50 * 1024 * 1024
         ),
         name="expert_exchange",
-    )(expert_of.reshape(1, count), tokens, w_gate, w_up, w_down)
+    )(pltpu.with_memory_space_constraint(expert_of.reshape(1, count), pltpu.HBM), tokens, w_gate, w_up, w_down)
 
 
 def solution(mesh):

time: 88.6 us -> 86.4 us (0.975); the launches traced: 87.1 us -> 86.2 us
    unnamed x3 -> x1, local copies, waits for them, and re-layouts: 2 us -> 1.32 us
where the time goes in v3:
time: 86.4 us; the launch traced here: 86.2 us
  Pallas kernels  84.9 us (98%)
  local copies, waits for them, and re-layouts  1.32 us (2%)
    pallas_call x1, Pallas kernels, shards(): pl.pallas_call(kernel, out_shape=jax.ShapeDtypeStruct((count, width), BF1...  84.9 us

profile of v3, /device:TPU:1, one launch (start us, length us, event | category | flops | bytes accessed | tf_op | source)
XLA Modules:
  0.0 86.2 jit_solution(15738170436425981196)
XLA Ops:
  0.0 84.9 %expert_exchange.1 = bf16[256,4096]{1,0:T(8,128)(2,1)S(1)} custom-call(s32[1,256]{1,0:T(1,128)} %bitcast.1, bf16[256,4096]{1,0:T(8,128)(2,1)} %tok_hbm.1, bf16[1,4096,768]{2,1,0:T(8,128)(2,1)} %wg_hbm.1, bf16[1,4096,768]{2,1,0:T(8,128)(2,1)} %wu_hbm.1, bf16[1,768,4096]{2,1,0:T(8,128)(2,1)} %wd_hbm.1), custom_call_target="tpu_custom_call" | custom-call | tf_op jit(solution)/shard_map/expert_exchange/pallas_call | solution.py:250
  84.9 1.3 %copy.7 = bf16[256,4096]{1,0:T(8,128)(2,1)} copy(bf16[256,4096]{1,0:T(8,128)(2,1)S(1)} %expert_exchange.1) | data formatting | bytes 4194304

commit v4 on v3

--- a/solution.py
+++ b/solution.py
@@ -20,7 +20,7 @@
 UNITS = DEVICES // UNIT
 GROUPS = ((0, 1, 2, 3), (4, 5, 6, 7))
 LANDINGS = ((0, 1, 2, 3), (4, 5, 6), (7,))
-AHEAD = 3
+NEAR, PLANES = 20, 48
 SPREAD = 1024
 
 
@@ -31,6 +31,11 @@
 def distance(off):
     dx, _, dz, dy = split(off)
     return sum(min(d, 4 - d) for d in (dx, dz, dy))
+
+
+def turns(off):
+    dx, _, dz, dy = split(off)
+    return (dx > 0) + (dz > 0) + (dy > 0)
 
 
 def even_order():
@@ -46,7 +51,8 @@
     rest, load, order = list(range(1, DEVICES)), [0] * 6, [0]
     while rest:
         rng.shuffle(rest)
-        best = min(rest, key=spread_of)
+        far = 1 if len(order) < NEAR else 2 if len(order) < PLANES else 3
+        best = min((off for off in rest if turns(off) <= far), key=spread_of)
         rest.remove(best)
         load = [a + b for a, b in zip(load, hops(best))]
         order.append(best)
@@ -72,6 +78,7 @@
     expert_hbm, tok_hbm, wg_hbm, wu_hbm, wd_hbm, mixed_ref,
     expert, tok, wg, wu, wd, rows, hid, place, turn, outgoing, parcel, result, returned,
     expert_sem, tok_sem, w_sem, send_sem, there_sem, back_send_sem, back_sem,
+    planes_sem, all_sem,
 ):
     pair, ep = lax.axis_index("pair"), lax.axis_index("ep")
     x, core, z, y = pair // 2, pair % 2, ep // 4, ep % 4
@@ -87,7 +94,7 @@
     tok_copy = pltpu.make_async_copy(tok_hbm, tok, tok_sem)
     tok_copy.start()
     barrier = pltpu.get_barrier_semaphore()
-    for k in sorted(range(1, DEVICES), key=lambda k: -distance(ORDER[k])):
+    for k in range(1, NEAR):
         pl.semaphore_signal(barrier, inc=1, device_id=peer(k, 1), device_id_type=MESH)
 
     count = tok.shape[0]
@@ -169,15 +176,26 @@
             ).astype(BF16)
 
     tok_copy.wait()
+    def tell(sem, offs):
+        for off in offs:
+            pl.semaphore_signal(
+                sem, inc=1, device_id=peer(ORDER.index(off), 1), device_id_type=MESH
+            )
+
     for u in range(UNITS):
         select(u)
         pack(rows, outgoing, u)
-        if u == AHEAD - 1:
-            pl.semaphore_wait(barrier, DEVICES - 1)
-            for v in range(AHEAD - 1):
-                send(there, v)
-        if u >= AHEAD:
+        if u == 0:
+            pl.semaphore_wait(barrier, NEAR - 1)
+            tell(planes_sem, [d * 4 for d in (1, 2, 3)] + [1, 2, 3])
+        elif u == 1:
+            send(there, 0)
+            pl.semaphore_wait(planes_sem, 6)
+            tell(all_sem, [d * 32 for d in (1, 2, 3)])
+        else:
             send(there, u - 1)
+            if u * UNIT == PLANES:
+                pl.semaphore_wait(all_sem, 3)
     send(there, UNITS - 1)
     parcel[:parcel_rows, :] = outgoing[:parcel_rows, :]
 
@@ -270,6 +288,8 @@
             pltpu.SemaphoreType.DMA((len(GROUPS),)),
             pltpu.SemaphoreType.DMA,
             pltpu.SemaphoreType.DMA((len(LANDINGS),)),
+            pltpu.SemaphoreType.REGULAR,
+            pltpu.SemaphoreType.REGULAR,
         ],
         compiler_params=pltpu.CompilerParams(
             collective_id=0, has_side_effects=True, vmem_limit_bytes=50 * 1024 * 1024

time: 86.4 us -> 84.7 us (0.980)
  Pallas kernels: 84.9 us -> 83.1 us
    pallas_call x1, Pallas kernels: 84.9 us -> 83.1 us  [shards(): pl.pallas_call(kernel, out_shape=jax.ShapeDtypeStruct((count, width), BF1...]
where the time goes in v4:
time: 84.7 us; the launch traced here: 84.5 us
  Pallas kernels  83.1 us (98%)
  local copies, waits for them, and re-layouts  1.32 us (2%)
    pallas_call x1, Pallas kernels, shards(): pl.pallas_call(kernel, out_shape=jax.ShapeDtypeStruct((count, width), BF1...  83.1 us

profile of v4, /device:TPU:1, one launch (start us, length us, event | category | flops | bytes accessed | tf_op | source)
XLA Modules:
  0.0 84.5 jit_solution(15615564209232058769)
XLA Ops:
  0.0 83.1 %expert_exchange.1 = bf16[256,4096]{1,0:T(8,128)(2,1)S(1)} custom-call(s32[1,256]{1,0:T(1,128)} %bitcast.1, bf16[256,4096]{1,0:T(8,128)(2,1)} %tok_hbm.1, bf16[1,4096,768]{2,1,0:T(8,128)(2,1)} %wg_hbm.1, bf16[1,4096,768]{2,1,0:T(8,128)(2,1)} %wu_hbm.1, bf16[1,768,4096]{2,1,0:T(8,128)(2,1)} %wd_hbm.1), custom_call_target="tpu_custom_call" | custom-call | tf_op jit(solution)/shard_map/expert_exchange/pallas_call | solution.py:268
  83.1 1.3 %copy.7 = bf16[256,4096]{1,0:T(8,128)(2,1)} copy(bf16[256,4096]{1,0:T(8,128)(2,1)S(1)} %expert_exchange.1) | data formatting | bytes 4194304

commit v5 on v4

--- a/solution.py
+++ b/solution.py
@@ -18,8 +18,8 @@
 SLOTS = UNIT * CAP
 BLOCKS = SLOTS // CUT
 UNITS = DEVICES // UNIT
-GROUPS = ((0, 1, 2, 3), (4, 5, 6, 7))
-LANDINGS = ((0, 1, 2, 3), (4, 5, 6), (7,))
+GROUPS = ((0, 1), (2, 3), (4, 5), (6, 7))
+LANDINGS = ((0, 1, 2, 3), (4, 5), (6,), (7,))
 NEAR, PLANES = 20, 48
 SPREAD = 1024
 
@@ -97,21 +97,25 @@
     for k in range(1, NEAR):
         pl.semaphore_signal(barrier, inc=1, device_id=peer(k, 1), device_id_type=MESH)
 
-    count = tok.shape[0]
-    expert_copy.wait()
-    row = expert[...]
-    down = lax.broadcasted_iota(jnp.int32, (count, count), 0)
-    across = lax.broadcasted_iota(jnp.int32, (count, count), 1)
-    column = jnp.sum(jnp.where(down == across, row, 0), axis=1, keepdims=True)
-    same = column == row
-    row_rank = jnp.sum(jnp.where(same & (down < across), 1, 0), axis=0, keepdims=True)
-    row_slot = step_of(row, x, core, z, y) * CAP + row_rank
     n = CUT * CUT
     turn_row = lax.broadcasted_iota(jnp.int32, (n, n), 0)
     turn_col = lax.broadcasted_iota(jnp.int32, (n, n), 1)
     turn[...] = jnp.where(
         (turn_row // CUT == turn_col % CUT) & (turn_row % CUT == turn_col // CUT), 1.0, 0.0
     ).astype(BF16)
+
+    count = tok.shape[0]
+    down = lax.broadcasted_iota(jnp.int32, (count, count), 0)
+    across = lax.broadcasted_iota(jnp.int32, (count, count), 1)
+    earlier = jnp.where(down < across, 1.0, 0.0).astype(BF16)
+    expert_copy.wait()
+    row = expert[...]
+    named = lax.broadcasted_iota(jnp.int32, (DEVICES, count), 0) == row
+    before = jnp.dot(
+        jnp.where(named, 1.0, 0.0).astype(BF16), earlier, preferred_element_type=F32
+    )
+    row_rank = jnp.sum(jnp.where(named, before, 0.0), axis=0, keepdims=True).astype(jnp.int32)
+    row_slot = step_of(row, x, core, z, y) * CAP + row_rank
 
     def pack(src, dst, unit):
         for b in range(unit * BLOCKS, (unit + 1) * BLOCKS):
@@ -184,18 +188,17 @@
 
     for u in range(UNITS):
         select(u)
+        if u > 0:
+            send(there, u - 1)
         pack(rows, outgoing, u)
         if u == 0:
             pl.semaphore_wait(barrier, NEAR - 1)
             tell(planes_sem, [d * 4 for d in (1, 2, 3)] + [1, 2, 3])
-        elif u == 1:
-            send(there, 0)
+        if u == 1:
             pl.semaphore_wait(planes_sem, 6)
             tell(all_sem, [d * 32 for d in (1, 2, 3)])
-        else:
-            send(there, u - 1)
-            if u * UNIT == PLANES:
-                pl.semaphore_wait(all_sem, 3)
+        if u * UNIT == PLANES:
+            pl.semaphore_wait(all_sem, 3)
     send(there, UNITS - 1)
     parcel[:parcel_rows, :] = outgoing[:parcel_rows, :]
 
@@ -240,7 +243,7 @@
         await_units(back, units)
         for u in units:
             unpack(returned, rows, u)
-        if units == LANDINGS[-2]:
+        if units == LANDINGS[0]:
             early = (units[-1] + 1) * SLOTS
 
             @spread
@@ -249,8 +252,8 @@
                     place[:, :early], rows[:early, at], preferred_element_type=F32
                 ).astype(BF16)
 
-    @spread
-    def _(at):
+    for c in range(0, tok.shape[1], SPREAD):
+        at = slice(c, c + SPREAD)
         late = jnp.dot(place[:, early:], rows[early:, at], preferred_element_type=F32)
         mixed_ref[:, at] = (mixed_ref[:, at].astype(F32) + late).astype(BF16)
 

time: 84.7 us -> 83.6 us (0.987)
  Pallas kernels: 83.1 us -> 82.1 us
    pallas_call x1, Pallas kernels: 83.1 us -> 82.1 us  [shards(): pl.pallas_call(kernel, out_shape=jax.ShapeDtypeStruct((count, width), BF1...]
where the time goes in v5:
time: 83.6 us; the launch traced here: 83.5 us
  Pallas kernels  82.1 us (98%)
  local copies, waits for them, and re-layouts  1.32 us (2%)
    pallas_call x1, Pallas kernels, shards(): pl.pallas_call(kernel, out_shape=jax.ShapeDtypeStruct((count, width), BF1...  82.1 us

profile of v5, /device:TPU:1, one launch (start us, length us, event | category | flops | bytes accessed | tf_op | source)
XLA Modules:
  0.0 83.5 jit_solution(13403297155701825063)
XLA Ops:
  0.0 82.1 %expert_exchange.1 = bf16[256,4096]{1,0:T(8,128)(2,1)S(1)} custom-call(s32[1,256]{1,0:T(1,128)} %bitcast.1, bf16[256,4096]{1,0:T(8,128)(2,1)} %tok_hbm.1, bf16[1,4096,768]{2,1,0:T(8,128)(2,1)} %wg_hbm.1, bf16[1,4096,768]{2,1,0:T(8,128)(2,1)} %wu_hbm.1, bf16[1,768,4096]{2,1,0:T(8,128)(2,1)} %wd_hbm.1), custom_call_target="tpu_custom_call" | custom-call | tf_op jit(solution)/shard_map/expert_exchange/pallas_call | solution.py:271
  82.1 1.3 %copy.7 = bf16[256,4096]{1,0:T(8,128)(2,1)} copy(bf16[256,4096]{1,0:T(8,128)(2,1)S(1)} %expert_exchange.1) | data formatting | bytes 4194304

commit v6 on v5

--- a/solution.py
+++ b/solution.py
@@ -20,7 +20,7 @@
 UNITS = DEVICES // UNIT
 GROUPS = ((0, 1), (2, 3), (4, 5), (6, 7))
 LANDINGS = ((0, 1, 2, 3), (4, 5), (6,), (7,))
-NEAR, PLANES = 20, 48
+NEAR, PLANES = 20, 32
 SPREAD = 1024
 
 

time: 83.6 us -> 83.4 us (level)
  no operation moved by 1% of the time
where the time goes in v6:
time: 83.4 us; the launch traced here: 83.1 us
  Pallas kernels  81.8 us (98%)
  local copies, waits for them, and re-layouts  1.32 us (2%)
    pallas_call x1, Pallas kernels, shards(): pl.pallas_call(kernel, out_shape=jax.ShapeDtypeStruct((count, width), BF1...  81.8 us

profile of v6, /device:TPU:1, one launch (start us, length us, event | category | flops | bytes accessed | tf_op | source)
XLA Modules:
  0.0 83.1 jit_solution(15278057276586387075)
XLA Ops:
  0.0 81.8 %expert_exchange.1 = bf16[256,4096]{1,0:T(8,128)(2,1)S(1)} custom-call(s32[1,256]{1,0:T(1,128)} %bitcast.1, bf16[256,4096]{1,0:T(8,128)(2,1)} %tok_hbm.1, bf16[1,4096,768]{2,1,0:T(8,128)(2,1)} %wg_hbm.1, bf16[1,4096,768]{2,1,0:T(8,128)(2,1)} %wu_hbm.1, bf16[1,768,4096]{2,1,0:T(8,128)(2,1)} %wd_hbm.1), custom_call_target="tpu_custom_call" | custom-call | tf_op jit(solution)/shard_map/expert_exchange/pallas_call | solution.py:271
  81.8 1.3 %copy.7 = bf16[256,4096]{1,0:T(8,128)(2,1)} copy(bf16[256,4096]{1,0:T(8,128)(2,1)S(1)} %expert_exchange.1) | data formatting | bytes 4194304
